TPU v7x, 128 devices: a whole 4x4x4 slice. The times are simulated.
128 devices in a mesh: dp: 8 (over z, core), mp: 16 (over x, y).
Axes of the slice: x: 4, y: 4, z: 4, core: 2. Of those that a mesh axis runs over, the one named last changes fastest.
Arguments:
- features: bfloat16 [8192, 2048], P('dp'), may hold values from -21 to 21
- rewards: float32 [32, 256], P('dp'), may hold values from -6 to 6
- old_values: float32 [32, 256], P('dp'), may hold values from -6 to 6
- dones: int32 [32, 256], P('dp'), may hold values 0 or 1
- lengths: int32 [32], P('dp'), may hold values from 128 to 256
- proj_weights: bfloat16 [2048, 2, 8192], P(None, None, 'mp'), may hold values from -0.125 to 0.125
- down_weight: bfloat16 [8192, 2048], P('mp'), may hold values from -0.0625 to 0.0625
- value_head: float32 [2048], replicated, may hold values from -0.0078125 to 0.0078125
- master: float32 [2048, 2, 8192], P('dp', None, 'mp'), may hold values from -0.125 to 0.125
- moment: float32 [2048, 2, 8192], P('dp', None, 'mp'), may hold values from -1.035801e-05 to 1.035801e-05
- second: float32 [2048, 2, 8192], P('dp', None, 'mp'), may hold values from 2.9802322e-13 to 2.9802322e-12
Outputs:
- master_new: float32 [2048, 2, 8192], P('dp', None, 'mp')
- moment_new: float32 [2048, 2, 8192], P('dp', None, 'mp')
- second_new: float32 [2048, 2, 8192], P('dp', None, 'mp')
- working: bfloat16 [2048, 2, 8192], P(None, None, 'mp')
- total_loss: float32 [], replicated
All inputs are finite; a program needn't handle non-finite values. No bound on the sum of `dones` on one device may be relied on, other than what follows from the above.
Results may differ from a plain program's by a relative error of at most 0.0011.
Values may be sent and summed in bfloat16 or wider, within the bound.
A program may use at most 128 MiB of HBM per device.

v0:
```python
import functools
import math
import jax
import jax.numpy as jnp
from jax import lax
from jax.sharding import Mesh
from jax.sharding import PartitionSpec as P

DP = ("dp_0", "dp_1")
MP = ("mp_0", "mp_1")
DP_MP = ("dp_0", "dp_1", "mp_0", "mp_1")
GAMMA = 0.99
LAMBDA = 0.95
MAX_NORM = 0.05


def own_block(parts, axes, sequence):
    shape = [lax.axis_size(a) for a in axes]
    parts = parts.reshape(*shape, *parts.shape[1:])
    parts = parts.transpose(*sequence, *range(len(axes), parts.ndim))
    parts = parts.reshape(-1, *parts.shape[len(axes) :])
    for k in sequence:
        parts = lax.psum_scatter(parts, axes[k], scatter_dimension=0, tiled=True)
    return parts[0]


def in_blocks(value, dim, count):
    before, after = (value.shape[:dim], value.shape[dim + 1 :])
    return jnp.moveaxis(value.reshape(*before, count, -1, *after), dim, 0)


def summed_rows(value, axes, sequence, dim):
    count = lax.axis_size(axes)
    return own_block(in_blocks(value, dim, count), axes, sequence)


def one_axis_at_a_time(value, axes):
    return functools.reduce(lax.psum, axes, value)


def gae_targets(rewards, old_values, dones, lengths):
    seq_len = rewards.shape[1]
    keeps = 1.0 - dones.astype(jnp.float32)
    following = jnp.concatenate([old_values[:, 1:], jnp.zeros_like(old_values[:, :1])], axis=1)
    deltas = rewards + GAMMA * following * keeps - old_values
    counted = jnp.cumsum(dones, axis=1) - dones
    places = jnp.arange(seq_len, dtype=jnp.int32)
    spans = places[None, :] - places[:, None]
    linked = (counted[:, :, None] == counted[:, None, :]) & (spans[None] >= 0)
    powers = jnp.exp(jnp.maximum(spans, 0).astype(jnp.float32) * math.log(GAMMA * LAMBDA))
    kernel = jnp.where(linked, powers[None], jnp.zeros((), jnp.float32))
    advantage = jnp.einsum("ats,as->at", kernel, deltas, precision=lax.Precision.HIGHEST)
    targets = (advantage + old_values).reshape(-1)
    mask = (places[None, :] < lengths[:, None]).astype(jnp.float32).reshape(-1)
    return (targets, mask)


def value_loss(features, mixed, targets, mask, value_head, total_tokens):
    stream = features.astype(jnp.float32) + mixed
    norm_factor = lax.rsqrt(jnp.mean(stream * stream, axis=-1) + 1e-05)
    normed = stream * norm_factor[:, None]
    estimate = jnp.dot(normed, value_head, precision=lax.Precision.HIGHEST)
    errors = estimate - targets
    loss_part = jnp.sum(mask * errors * errors) / total_tokens
    coeff = 2.0 * mask * errors / total_tokens
    head_grad = coeff[:, None] * value_head[None, :]
    out_grad = (
        norm_factor[:, None]
        * (head_grad - normed * jnp.mean(head_grad * normed, axis=-1, keepdims=True))
    ).astype(jnp.bfloat16)
    return (loss_part, out_grad)


def contract_rows(left, right):
    return lax.dot_general(
        left, right, (((0,), (0,)), ((), ())), preferred_element_type=jnp.float32
    )


def per_device(
    features,
    rewards,
    old_values,
    dones,
    lengths,
    proj_weights,
    down_weight,
    value_head,
    master,
    moment,
    second,
):
    token_count = features.shape[0]
    model_width = features.shape[1]
    ff_local = down_weight.shape[0]
    data_ways = lax.axis_size(DP)
    model_ways = lax.axis_size(MP)
    total_tokens = token_count * data_ways
    targets, mask = gae_targets(rewards, old_values, dones, lengths)
    both = jnp.dot(
        features,
        proj_weights.reshape(model_width, 2 * ff_local),
        preferred_element_type=jnp.float32,
    )
    both = both.reshape(token_count, 2, ff_local)
    gate_values = both[:, 0, :]
    up_values = both[:, 1, :]
    hidden = (jax.nn.silu(gate_values) * up_values).astype(jnp.bfloat16)
    mixed = lax.psum(
        jnp.dot(hidden, down_weight, preferred_element_type=jnp.float32).astype(jnp.bfloat16), MP
    ).astype(jnp.float32)
    loss_part, out_grad = value_loss(features, mixed, targets, mask, value_head, total_tokens)
    loss_part = loss_part / model_ways
    hidden_grad = jnp.dot(out_grad, down_weight.T, preferred_element_type=jnp.float32)
    gate_sigmoid = jax.nn.sigmoid(gate_values)
    gate_grad = (
        hidden_grad * up_values * gate_sigmoid * (1.0 + gate_values * (1.0 - gate_sigmoid))
    ).astype(jnp.bfloat16)
    up_grad = (hidden_grad * gate_values * gate_sigmoid).astype(jnp.bfloat16)
    both_grad = jnp.stack([gate_grad, up_grad], axis=1).reshape(token_count, 2 * ff_local)
    row_share = model_width // data_ways
    grads = summed_rows(
        contract_rows(features, both_grad).reshape(row_share * lax.axis_size(DP), 2, ff_local),
        DP,
        (1, 0),
        0,
    )
    squares = jnp.sum(grads * grads)
    squared_total, total_loss = (
        one_axis_at_a_time(squares, DP_MP),
        one_axis_at_a_time(loss_part, DP_MP),
    )
    clip = jnp.minimum(1.0, MAX_NORM / (jnp.sqrt(squared_total) + 1e-06))
    clipped = clip * grads
    moment_new = 0.9 * moment + 0.1 * clipped
    second_new = 0.999 * second + 0.001 * clipped * clipped
    first_hat = moment_new / (1.0 - 0.9**10)
    second_hat = second_new / (1.0 - 0.999**10)
    master_new = master - 0.001 * (first_hat / (jnp.sqrt(second_hat) + 1e-08) + 0.1 * master)
    working = lax.all_gather(master_new.astype(jnp.bfloat16), DP, axis=0, tiled=True)
    return (master_new, moment_new, second_new, working, total_loss)


def solution(mesh):
    finer = Mesh(mesh.devices.reshape(4, 2, 4, 4), ("dp_0", "dp_1", "mp_0", "mp_1"))
    return jax.shard_map(
        per_device,
        mesh=finer,
        in_specs=(
            P(DP, None),
            P(DP, None),
            P(DP, None),
            P(DP, None),
            P(DP),
            P(None, None, MP),
            P(MP, None),
            P(),
            P(DP, None, MP),
            P(DP, None, MP),
            P(DP, None, MP),
        ),
        out_specs=(P(DP, None, MP), P(DP, None, MP), P(DP, None, MP), P(None, None, MP), P()),
        check_vma=False,
    )
```

profile of v0, /device:TPU:1, one launch (start us, length us, event | category | flops | bytes accessed | tf_op | source)
XLA Modules:
  0.0 348.5 jit_solution(17223176488133655442)
XLA Ops:
  7.2 5.5 %copy.34 = bf16[256,8,2,512]{3,1,2,0:T(8,128)(2,1)} copy(bf16[256,8,2,512]{3,2,1,0:T(2,128)(2,1)} %bitcast.73) | data formatting | bytes 8388608
  12.8 6.5 %copy.21 = bf16[1024,2048]{1,0:T(8,128)(2,1)} copy(bf16[1024,2048]{0,1:T(8,128)(2,1)} %bitcast.72) | data formatting | bytes 8388608 | tf_op jit(solution)/shard_map/dot_general | solution.py:100
  19.3 7.6 %fusion.6 = f32[1024,2,512]{0,2,1:T(8,128)S(1)} fusion(bf16[2,512,2048]{2,1,0:T(8,128)(2,1)} %bitcast.74, bf16[1024,2048]{1,0:T(8,128)(2,1)} %param.11), kind=kOutput, calls=%fused_computation.10 | convolution fusion | flops 4294967296 | bytes 12582912 | tf_op jit(solution)/shard_map/dot_general | solution.py:100
  26.9 2.0 copy-done.9
  28.9 4.4 %convolution_convert_fusion = bf16[1024,2048]{1,0:T(8,128)(2,1)} fusion(bf16[512,2048]{1,0:T(8,128)(2,1)S(1)} %copy-done, f32[1024,2,512]{0,2,1:T(8,128)S(1)} %fusion.6), kind=kOutput, calls=%fused_computation.14 | convolution fusion | flops 2152726528 | bytes 10485760 | tf_op jit(solution)/shard_map/dot_general | solution.py:110
  37.1 102.5 %all-reduce.7.cloned.1.call-done = bf16[1024,2048]{1,0:T(8,128)(2,1)} async-done(((bf16[1024,2048]{1,0:T(8,128)(2,1)}), bf16[1024,2048]{1,0:T(8,128)(2,1)}) %all-reduce.7.cloned.1.call-update) | async-done | bytes 4194320 | tf_op jit(solution)/shard_map/psum | solution.py:109
  139.7 5.0 %multiply_reduce_fusion = f32[1024]{0:T(1024)S(1)} fusion(bf16[1024,2048]{1,0:T(8,128)(2,1)} %all-reduce.7.cloned.1.call-done, bf16[1024,2048]{1,0:T(8,128)(2,1)} %param.11), kind=kLoop, calls=%fused_computation.5 | loop fusion | flops 10484736 | bytes 8392704 | tf_op jit(solution)/shard_map/reduce_sum | solution.py:60
  145.6 8.1 %fusion.4 = f32[1,1024]{1,0:T(1,128)S(1)} fusion(f32[2048,1]{0,1:T(1,128)S(1)} %bitcast.76, bf16[1024,2048]{1,0:T(8,128)(2,1)S(1)} %copy-done.3, bf16[1024,2048]{1,0:T(8,128)(2,1)S(1)} %copy-done.2, f32[1024]{0:T(1024)S(1)} %add_rsqrt_fusion), kind=kOutput, calls=%fused_computation.8 | convolution fusion | flops 33554432 | bytes 8404992 | tf_op jit(solution)/shard_map/dot_general | solution.py:62
  154.4 2.6 fusion
  156.9 5.4 %fusion.19 = (bf16[1024,1,512]{0,2,1:T(8,128)(2,1)S(1)}, bf16[1024,1,512]{0,2,1:T(8,128)(2,1)S(1)}) fusion(f32[1024,2,512]{0,2,1:T(8,128)S(1)} %copy-done.10, bf16[512,2048]{1,0:T(8,128)(2,1)S(1)} %copy-done, bf16[1024,2048]{1,0:T(8,128)(2,1)S(1)} %copy-done.3, bf16[1024,2048]{1,0:T(8,128)(2,1)S(1)} %copy-done.2, f32[1024]{0:T(1024)S(1)} %broadcast_multiply_fusion, ...), kind=kOutput, calls=%fused_computation.36 | convolution fusion | flops 2173173760 | bytes 16797696 | tf_op jit(solution)/shard_map/dot_general | solution.py:114
  162.6 6.7 %convolution_bitcast_fusion = f32[2048,1024]{0,1:T(8,128)} fusion(bf16[1024,1024]{0,1:T(8,128)(2,1)S(1)} %bitcast.75, bf16[1024,2048]{1,0:T(8,128)(2,1)S(1)} %copy-done.2), kind=kOutput, calls=%fused_computation.9 | convolution fusion | flops 4294967296 | bytes 14680064 | tf_op jit(solution)/shard_map/dot_general | solution.py:75
  169.3 11.7 %reshape_reshape_reshape.3 = f32[4,2,256,2,512]{2,1,0,4,3:T(2,128)} reshape(f32[2048,1024]{0,1:T(8,128)} %convolution_bitcast_fusion) | data formatting | bytes 16777216 | tf_op jit(solution)/shard_map/reshape;reshape;reshape | solution.py:19
  181.0 13.1 %copy.24 = f32[2,4,256,2,512]{4,2,3,1,0:T(8,128)} copy(f32[2,4,256,2,512]{2,0,1,4,3:T(2,128)} %bitcast.71) | data formatting | bytes 16777216 | tf_op jit(solution)/shard_map/transpose | solution.py:20
  194.2 19.7 %reduce-scatter.3.cloned.1.call-done = f32[4,256,2,512]{3,1,2,0:T(8,128)} async-done(((f32[8,256,2,512]{3,1,2,0:T(8,128)}), f32[4,256,2,512]{3,1,2,0:T(8,128)}) %reduce-scatter.3.cloned.1.call-update) | async-done | bytes 4194320 | tf_op jit(solution)/shard_map/reduce_scatter | solution.py:23
  214.6 49.8 %reduce-scatter.5.cloned.1.call-done = f32[1,256,2,512]{3,1,2,0:T(8,128)} async-done(((f32[4,256,2,512]{3,1,2,0:T(8,128)}), f32[1,256,2,512]{3,1,2,0:T(8,128)}) %reduce-scatter.5.cloned.1.call-update) | async-done | bytes 1048592 | tf_op jit(solution)/shard_map/reduce_scatter | solution.py:23
  264.4 2.1 multiply_reduce_fusion.1
  266.5 7.1 %all-reduce.3 = (f32[]{:T(128)}, f32[]{:T(128)}) all-reduce(f32[]{:T(128)} %multiply_reduce_fusion.1, f32[]{:T(128)S(6)} %div.55), channel_id=1, replica_groups=mesh['dp_0'=4,'dp_1'=2,'mp_0'=4,'mp_1'=4] {'dp_0'}, use_global_device_ids=true, to_apply=%region_8.9 | all-reduce | flops 2 | bytes 16 | tf_op jit(solution)/shard_map/psum | solution.py:38
  273.6 5.5 %all-reduce.4 = (f32[]{:T(128)}, f32[]{:T(128)}) all-reduce(f32[]{:T(128)} %get-tuple-element.14, f32[]{:T(128)} %get-tuple-element.15), channel_id=1, replica_groups=mesh['dp_0'=4,'dp_1'=2,'mp_0'=4,'mp_1'=4] {'dp_1'}, use_global_device_ids=true, to_apply=%region_9.10 | all-reduce | flops 2 | bytes 16 | tf_op jit(solution)/shard_map/psum | solution.py:38
  279.1 9.0 %all-reduce.2 = (f32[]{:T(128)}, f32[]{:T(128)}) all-reduce(f32[]{:T(128)} %get-tuple-element.16, f32[]{:T(128)} %get-tuple-element.17), channel_id=1, replica_groups=mesh['dp_0'=4,'dp_1'=2,'mp_0'=4,'mp_1'=4] {'mp_0'}, use_global_device_ids=true, to_apply=%region_10.11 | all-reduce | flops 2 | bytes 16 | tf_op jit(solution)/shard_map/psum | solution.py:38
  288.1 9.1 %all-reduce.1 = (f32[]{:T(128)}, f32[]{:T(128)}) all-reduce(f32[]{:T(128)} %get-tuple-element.12, f32[]{:T(128)} %get-tuple-element.13), channel_id=1, replica_groups=mesh['dp_0'=4,'dp_1'=2,'mp_0'=4,'mp_1'=4] {'mp_1'}, use_global_device_ids=true, to_apply=%region_11.12 | all-reduce | flops 2 | bytes 16 | tf_op jit(solution)/shard_map/psum | solution.py:38
  297.9 3.2 fusion.31
  302.5 1.8 copy.29
  307.8 26.3 %all-gather.2.cloned.1.call-done = bf16[2048,2,512]{2,1,0:T(2,128)(2,1)} async-done(((bf16[256,2,512]{2,1,0:T(2,128)(2,1)}), bf16[2048,2,512]{2,1,0:T(2,128)(2,1)}) %all-gather.2.cloned.1.call-update) | async-done | bytes 4194320 | tf_op jit(solution)/shard_map/all_gather | solution.py:140
  334.1 7.8 %copy.53 = bf16[2048,2,512]{2,1,0:T(2,128)(2,1)} copy(bf16[2048,2,512]{2,1,0:T(2,128)(2,1)} %all-gather.2.cloned.1.call-done) | data formatting | bytes 8388608
  (54 shorter events, 10.5 us)
Async XLA Ops:
  7.2 21.7 %copy-start = (bf16[512,2048]{1,0:T(8,128)(2,1)S(1)}, bf16[512,2048]{1,0:T(8,128)(2,1)}, u32[]{:S(2)}) copy-start(bf16[512,2048]{1,0:T(8,128)(2,1)} %param.17) | copy-start | bytes 6291460
  7.2 132.5 %all-reduce.7.cloned.1.call-start = ((), (), s32[]{:S(2)}) async-start(), calls=%async_computation.2 | async-start | bytes 8388608 | tf_op jit(solution)/shard_map/psum | solution.py:109
  26.9 2.0 copy-start.9
  33.3 0.7 copy-start.8
  33.3 0.7 copy-start.5
  33.3 0.8 copy-start.4
  33.3 2.5 copy-start.7
  33.4 180.5 %reduce-scatter.3.cloned.1.call-start = ((), (), s32[]{:S(2)}) async-start(), calls=%async_computation.3 | async-start | bytes 12582912 | tf_op jit(solution)/shard_map/reduce_scatter | solution.py:23
  37.1 107.6 %copy-start.6 = (f32[2048]{0:T(1024)S(1)}, f32[2048]{0:T(1024)}, u32[]{:S(2)}) copy-start(f32[2048]{0:T(1024)} %param.18) | copy-start | bytes 24580
  139.7 5.1 %copy-start.2 = (bf16[1024,2048]{1,0:T(8,128)(2,1)S(1)}, bf16[1024,2048]{1,0:T(8,128)(2,1)}, u32[]{:S(2)}) copy-start(bf16[1024,2048]{1,0:T(8,128)(2,1)} %param.11) | copy-start | bytes 12582916
  139.7 5.9 %copy-start.3 = (bf16[1024,2048]{1,0:T(8,128)(2,1)S(1)}, bf16[1024,2048]{1,0:T(8,128)(2,1)}, u32[]{:S(2)}) copy-start(bf16[1024,2048]{1,0:T(8,128)(2,1)} %all-reduce.7.cloned.1.call-done) | copy-start | bytes 12582916
  154.3 2.6 copy-start.10
  194.1 70.3 %reduce-scatter.5.cloned.1.call-start = ((), (), s32[]{:S(2)}) async-start(), calls=%async_computation.4 | async-start | bytes 5242880 | tf_op jit(solution)/shard_map/reduce_scatter | solution.py:23
  213.9 120.2 %all-gather.2.cloned.1.call-start = ((), (), s32[]{:S(2)}) async-start(), calls=%async_computation.5 | async-start | bytes 4718592 | tf_op jit(solution)/shard_map/all_gather | solution.py:140
  334.1 7.9 %copy-start.1 = (bf16[512,2048]{1,0:T(8,128)(2,1)S(1)}, bf16[512,2048]{1,0:T(8,128)(2,1)}, u32[]{:S(2)}) copy-start(bf16[512,2048]{1,0:T(8,128)(2,1)} %param.17) | copy-start | bytes 6291460
Sparse Core Ops, SparseCore 0:
  33.5 106.1 all-reduce.6
  194.2 19.5 reduce-scatter.2
  216.3 48.0 reduce-scatter.4
  302.6 31.4 all-gather.1
where the time goes:
time: 350 us; the launch traced here: 348 us
  waiting for transfers between devices  198 us (57%)
  local copies, waits for them, and re-layouts  55.1 us (16%)
  matrix products  33.5 us (10%)
  blocking collectives  30.7 us (9%)
  other arithmetic  15.3 us (4%)
  between operations  15.3 us (4%)
    psum x1, waiting for transfers between devices, per_device(): lax.psum(jnp.dot(hidden, down_weight, preferred_element_type=jnp.float32)...  103 us
    reduce_scatter x2, waiting for transfers between devices, own_block(): parts = lax.psum_scatter(parts, axes[k], scatter_dimension=0, tiled=True)  69.5 us
    psum x4, blocking collectives, one_axis_at_a_time(): return functools.reduce(lax.psum, axes, value)  30.7 us
    all_gather x1, waiting for transfers between devices, per_device(): lax.all_gather(master_new.astype(jnp.bfloat16), DP, axis=0, tiled=True)  26.3 us
    unnamed x28, local copies, waits for them, and re-layouts  22 us
    transpose x1, local copies, waits for them, and re-layouts, own_block(): parts = parts.transpose(*sequence, *range(len(axes), parts.ndim))  13.1 us
    another operation x1, local copies, waits for them, and re-layouts, own_block(): parts = parts.reshape(*shape, *parts.shape[1:])  11.7 us
    dot_general x1, matrix products, value_loss(): estimate = jnp.dot(normed, value_head, precision=lax.Precision.HIGHEST)  8.13 us
  transfers between devices with their start and end apart: 4, of which 4 were waited for; matrix products, arithmetic and copies ran while one was open for 2% of the time, Pallas kernels for 0%

commit v1 on v0

--- a/solution.py
+++ b/solution.py
@@ -12,6 +12,11 @@
 GAMMA = 0.99
 LAMBDA = 0.95
 MAX_NORM = 0.05
+
+
+def summed_here(block, mesh_axis):
+    terms = lax.all_gather(block, mesh_axis)
+    return jnp.sum(terms, axis=0)
 
 
 def own_block(parts, axes, sequence):
@@ -106,7 +111,7 @@
     gate_values = both[:, 0, :]
     up_values = both[:, 1, :]
     hidden = (jax.nn.silu(gate_values) * up_values).astype(jnp.bfloat16)
-    mixed = lax.psum(
+    mixed = summed_here(
         jnp.dot(hidden, down_weight, preferred_element_type=jnp.float32).astype(jnp.bfloat16), MP
     ).astype(jnp.float32)
     loss_part, out_grad = value_loss(features, mixed, targets, mask, value_head, total_tokens)

time: 350 us -> 638 us (1.82)
  waiting for transfers between devices: 198 us -> 463 us
  other arithmetic: 15.3 us -> 39 us
    all_gather x0 -> x1, waiting for transfers between devices: none -> 368 us  [summed_here(): terms = lax.all_gather(block, mesh_axis)]
    psum x1 -> x0, waiting for transfers between devices: 103 us -> none  [per_device(): lax.psum(jnp.dot(hidden, down_weight, preferred_element_type=jnp.float32)...]
    reduce_sum x0 -> x1, other arithmetic: none -> 23.7 us  [summed_here(): return jnp.sum(terms, axis=0)]
  transfers between devices with their start and end apart: 4 -> 4, of which waited for: 4 -> 4; matrix products, arithmetic and copies ran while one was open for 2% -> 1% of each run, Pallas kernels for 0% -> 0%
where the time goes in v1:
time: 638 us; the launch traced here: 637 us
  waiting for transfers between devices  463 us (73%)
  local copies, waits for them, and re-layouts  55.1 us (9%)
  other arithmetic  39 us (6%)
  matrix products  33.2 us (5%)
  blocking collectives  30.7 us (5%)
  between operations  15.3 us (2%)
    all_gather x1, waiting for transfers between devices, summed_here(): terms = lax.all_gather(block, mesh_axis)  368 us
    reduce_scatter x2, waiting for transfers between devices, own_block(): parts = lax.psum_scatter(parts, axes[k], scatter_dimension=0, tiled=True)  69.2 us
    psum x4, blocking collectives, one_axis_at_a_time(): return functools.reduce(lax.psum, axes, value)  30.7 us
    all_gather x1, waiting for transfers between devices, per_device(): lax.all_gather(master_new.astype(jnp.bfloat16), DP, axis=0, tiled=True)  26.3 us
    reduce_sum x1, other arithmetic, summed_here(): return jnp.sum(terms, axis=0)  23.7 us
    unnamed x28, local copies, waits for them, and re-layouts  22.1 us
    transpose x1, local copies, waits for them, and re-layouts, own_block(): parts = parts.transpose(*sequence, *range(len(axes), parts.ndim))  13.1 us
  transfers between devices with their start and end apart: 4, of which 4 were waited for; matrix products, arithmetic and copies ran while one was open for 1% of the time, Pallas kernels for 0%

profile of v1, /device:TPU:1, one launch (start us, length us, event | category | flops | bytes accessed | tf_op | source)
XLA Modules:
  0.0 637.0 jit_solution(14763888266237457050)
XLA Ops:
  7.2 5.5 copy.34
  12.8 6.5 %copy.21 = bf16[1024,2048]{1,0:T(8,128)(2,1)} copy(bf16[1024,2048]{0,1:T(8,128)(2,1)} %bitcast.73) | data formatting | bytes 8388608 | tf_op jit(solution)/shard_map/dot_general | solution.py:105
  19.3 7.6 %fusion.6 = f32[1024,2,512]{0,2,1:T(8,128)S(1)} fusion(bf16[2,512,2048]{2,1,0:T(8,128)(2,1)} %bitcast.75, bf16[1024,2048]{1,0:T(8,128)(2,1)} %param.11), kind=kOutput, calls=%fused_computation.10 | convolution fusion | flops 4294967296 | bytes 12582912 | tf_op jit(solution)/shard_map/dot_general | solution.py:105
  26.9 2.0 copy-done.9
  28.9 4.4 convolution_convert_fusion
  37.2 367.8 %all-gather.6.cloned.1.call-done = bf16[16384,2048]{1,0:T(8,128)(2,1)} async-done(((bf16[1024,2048]{1,0:T(8,128)(2,1)}), bf16[16384,2048]{1,0:T(8,128)(2,1)}) %all-gather.6.cloned.1.call-update) | async-done | bytes 67108880 | tf_op jit(solution)/shard_map/all_gather | solution.py:18
  404.9 23.7 %reduce_sum.48 = bf16[1024,2048]{1,0:T(8,128)(2,1)} reduce(bf16[16,1024,2048]{2,1,0:T(8,128)(2,1)} %bitcast.5, bf16[]{:T(256)} %constant.23.clone.1), dimensions={0}, to_apply=%region_0.0 | reduce | flops 31457280 | bytes 71303168 | tf_op jit(solution)/shard_map/reduce_sum | solution.py:19
  428.7 5.0 multiply_reduce_fusion
  434.6 8.1 %fusion.4 = f32[1,1024]{1,0:T(1,128)S(1)} fusion(f32[2048,1]{0,1:T(1,128)S(1)} %bitcast.77, bf16[1024,2048]{1,0:T(8,128)(2,1)S(1)} %copy-done.2, bf16[1024,2048]{1,0:T(8,128)(2,1)S(1)} %copy-done.3, f32[1024]{0:T(1024)S(1)} %add_rsqrt_fusion), kind=kOutput, calls=%fused_computation.8 | convolution fusion | flops 33554432 | bytes 8404992 | tf_op jit(solution)/shard_map/dot_general | solution.py:67
  443.4 2.5 fusion
  445.9 5.2 fusion.19
  451.3 6.7 %convolution_bitcast_fusion = f32[2048,1024]{0,1:T(8,128)} fusion(bf16[1024,1024]{0,1:T(8,128)(2,1)S(1)} %bitcast.76, bf16[1024,2048]{1,0:T(8,128)(2,1)S(1)} %copy-done.3), kind=kOutput, calls=%fused_computation.9 | convolution fusion | flops 4294967296 | bytes 14680064 | tf_op jit(solution)/shard_map/dot_general | solution.py:80
  458.0 11.7 %reshape_reshape_reshape.3 = f32[4,2,256,2,512]{2,1,0,4,3:T(2,128)} reshape(f32[2048,1024]{0,1:T(8,128)} %convolution_bitcast_fusion) | data formatting | bytes 16777216 | tf_op jit(solution)/shard_map/reshape;reshape;reshape | solution.py:24
  469.7 13.1 %copy.24 = f32[2,4,256,2,512]{4,2,3,1,0:T(8,128)} copy(f32[2,4,256,2,512]{2,0,1,4,3:T(2,128)} %bitcast.72) | data formatting | bytes 16777216 | tf_op jit(solution)/shard_map/transpose | solution.py:25
  482.9 19.5 %reduce-scatter.3.cloned.1.call-done = f32[4,256,2,512]{3,1,2,0:T(8,128)} async-done(((f32[8,256,2,512]{3,1,2,0:T(8,128)}), f32[4,256,2,512]{3,1,2,0:T(8,128)}) %reduce-scatter.3.cloned.1.call-update) | async-done | bytes 4194320 | tf_op jit(solution)/shard_map/reduce_scatter | solution.py:28
  503.1 49.8 %reduce-scatter.5.cloned.1.call-done = f32[1,256,2,512]{3,1,2,0:T(8,128)} async-done(((f32[4,256,2,512]{3,1,2,0:T(8,128)}), f32[1,256,2,512]{3,1,2,0:T(8,128)}) %reduce-scatter.5.cloned.1.call-update) | async-done | bytes 1048592 | tf_op jit(solution)/shard_map/reduce_scatter | solution.py:28
  552.9 2.1 multiply_reduce_fusion.1
  555.0 7.1 %all-reduce.3 = (f32[]{:T(128)}, f32[]{:T(128)}) all-reduce(f32[]{:T(128)} %multiply_reduce_fusion.1, f32[]{:T(128)S(6)} %div.55), channel_id=1, replica_groups=mesh['dp_0'=4,'dp_1'=2,'mp_0'=4,'mp_1'=4] {'dp_0'}, use_global_device_ids=true, to_apply=%region_8.9 | all-reduce | flops 2 | bytes 16 | tf_op jit(solution)/shard_map/psum | solution.py:43
  562.1 5.5 all-reduce.4
  567.6 9.0 %all-reduce.2 = (f32[]{:T(128)}, f32[]{:T(128)}) all-reduce(f32[]{:T(128)} %get-tuple-element.16, f32[]{:T(128)} %get-tuple-element.17), channel_id=1, replica_groups=mesh['dp_0'=4,'dp_1'=2,'mp_0'=4,'mp_1'=4] {'mp_0'}, use_global_device_ids=true, to_apply=%region_10.11 | all-reduce | flops 2 | bytes 16 | tf_op jit(solution)/shard_map/psum | solution.py:43
  576.6 9.1 %all-reduce.1 = (f32[]{:T(128)}, f32[]{:T(128)}) all-reduce(f32[]{:T(128)} %get-tuple-element.12, f32[]{:T(128)} %get-tuple-element.13), channel_id=1, replica_groups=mesh['dp_0'=4,'dp_1'=2,'mp_0'=4,'mp_1'=4] {'mp_1'}, use_global_device_ids=true, to_apply=%region_11.12 | all-reduce | flops 2 | bytes 16 | tf_op jit(solution)/shard_map/psum | solution.py:43
  586.4 3.2 fusion.31
  596.3 26.3 %all-gather.4.cloned.1.call-done = bf16[2048,2,512]{2,1,0:T(2,128)(2,1)} async-done(((bf16[256,2,512]{2,1,0:T(2,128)(2,1)}), bf16[2048,2,512]{2,1,0:T(2,128)(2,1)}) %all-gather.4.cloned.1.call-update) | async-done | bytes 4194320 | tf_op jit(solution)/shard_map/all_gather | solution.py:145
  622.6 7.8 %copy.52 = bf16[2048,2,512]{2,1,0:T(2,128)(2,1)} copy(bf16[2048,2,512]{2,1,0:T(2,128)(2,1)} %all-gather.4.cloned.1.call-done) | data formatting | bytes 8388608
  (55 shorter events, 12.3 us)
Async XLA Ops:
  7.2 21.7 %copy-start = (bf16[512,2048]{1,0:T(8,128)(2,1)S(1)}, bf16[512,2048]{1,0:T(8,128)(2,1)}, u32[]{:S(2)}) copy-start(bf16[512,2048]{1,0:T(8,128)(2,1)} %param.17) | copy-start | bytes 6291460
  7.2 397.7 %all-gather.6.cloned.1.call-start = ((), (), s32[]{:S(2)}) async-start(), calls=%async_computation.5 | async-start | bytes 71303168 | tf_op jit(solution)/shard_map/all_gather | solution.py:18
  26.9 2.0 copy-start.9
  33.3 0.7 copy-start.4
  33.3 2.2 copy-start.5
  33.3 2.5 copy-start.7
  33.3 3.7 copy-start.8
  33.4 469.0 %reduce-scatter.3.cloned.1.call-start = ((), (), s32[]{:S(2)}) async-start(), calls=%async_computation.2 | async-start | bytes 12582912 | tf_op jit(solution)/shard_map/reduce_scatter | solution.py:28
  428.7 5.0 copy-start.2
  428.7 5.9 copy-start.3
  428.7 5.9 copy-start.6
  443.3 2.6 copy-start.10
  482.8 70.0 %reduce-scatter.5.cloned.1.call-start = ((), (), s32[]{:S(2)}) async-start(), calls=%async_computation.3 | async-start | bytes 5242880 | tf_op jit(solution)/shard_map/reduce_scatter | solution.py:28
  502.4 120.2 %all-gather.4.cloned.1.call-start = ((), (), s32[]{:S(2)}) async-start(), calls=%async_computation.4 | async-start | bytes 4718592 | tf_op jit(solution)/shard_map/all_gather | solution.py:145
  622.6 7.9 %copy-start.1 = (bf16[512,2048]{1,0:T(8,128)(2,1)S(1)}, bf16[512,2048]{1,0:T(8,128)(2,1)}, u32[]{:S(2)}) copy-start(bf16[512,2048]{1,0:T(8,128)(2,1)} %param.17) | copy-start | bytes 6291460
Sparse Core Ops, SparseCore 0:
  33.5 371.4 all-gather.5
  483.0 19.3 reduce-scatter.2
  504.8 48.0 reduce-scatter.4
  591.1 31.4 all-gather.3
